TPU v7x, 32 devices: a whole 2x2x4 slice. The times are simulated.
32 devices in a mesh: sfc: 32 (over z, y, x, core).
Axes of the slice: x: 2, y: 2, z: 4, core: 2. Of those that a mesh axis runs over, the one named last changes fastest.
Arguments:
- tracers: float32 [2048, 3, 480], P('sfc'), may hold values from -6 to 6
- weights: float32 [2, 2048, 3, 256], P(None, 'sfc'), may hold values from -1.5 to 1.5
- departure: int32 [2048, 48], P('sfc'), may hold values from 0 to 95, as said below
- needs: int32 [32, 8, 4], P('sfc'), may hold values from 0 to 63
- counts: int32 [32, 8], P('sfc'), may hold values from 1 to 4, as said below
Outputs:
- mixed: float32 [2048, 3, 480], P('sfc')
Inputs may be any that keep to these rules, and one draw needn't show every extreme that they name: `departure`: each entry is a slot of its range's source table: below 64 a local element; otherwise 64 + j * 4 + c with c below counts[r, j] of its range r. `counts`: some range uses all 4 entries of every list in every draw.
All inputs are finite; a program needn't handle non-finite values.
Results may differ from a plain program's by a relative error of at most 0.0003.
Values sent between devices are 32-bit elements; how exact they have to be, the bound alone decides.
A program may use at most 64 MiB of HBM per device.

v0:
```python
import functools

import jax
import jax.numpy as jnp
from jax import lax
from jax.experimental import pallas as pl
from jax.experimental.pallas import tpu as pltpu
from jax.sharding import PartitionSpec as P

NODES = 16
TRACERS = 30
PADDED = 32
MESH = pl.DeviceIdType.MESH
F32 = jnp.float32
BF16 = jnp.bfloat16


def high_part(value):
    return value.astype(BF16).astype(F32)


def transposed_dot(a, b):
    return lax.dot_general(a, b, (((1,), (1,)), ((), ())), preferred_element_type=F32)


def kernel(
    tracers_far, weights_far, departure_far, needs, counts, out_far,
    tracers, weights, departure, out, table, picks, mats, slot_ids, wish, asked, rows, rows_asked, sent, got,
    spread, same, wish_send, wish_got, row_send, row_got, loaded, stored,
):
    count = lax.axis_size("sfc")
    me = lax.axis_index("sfc")
    substeps, levels, elements, _ = weights.shape
    sides, cap = asked.shape[0], asked.shape[1]
    reach = sides // 2
    offsets = [j - reach if j < reach else j - reach + 1 for j in range(sides)]
    wide = NODES * PADDED
    narrow = NODES * TRACERS
    remote = sides * cap
    half = NODES // 2
    own_lanes = 2 * elements

    def device(offset):
        return (lax.rem(me + offset + count, count),)

    barrier = pltpu.get_barrier_semaphore()
    for o in offsets:
        pl.semaphore_signal(barrier, inc=1, device_id=device(o), device_id_type=MESH)

    loads = [
        pltpu.make_async_copy(far, near, loaded.at[i])
        for i, (far, near) in enumerate(((tracers_far, tracers), (departure_far, departure), (weights_far, weights)))
    ]
    for load in loads:
        load.start()

    for j in range(sides):
        for c in range(cap):
            wish[j, c : c + 1, :] = jnp.full((1, 128), needs[0, c, j], jnp.int32)

    pl.semaphore_wait(barrier, sides)

    wishes = []
    for j, o in enumerate(offsets):
        copy = pltpu.make_async_remote_copy(
            src_ref=wish.at[j], dst_ref=asked.at[j],
            send_sem=wish_send.at[j], recv_sem=wish_got.at[j],
            device_id=device(o), device_id_type=MESH,
        )
        copy.start()
        wishes.append(copy)

    def row_copy(s, l, j):
        return pltpu.make_async_remote_copy(
            src_ref=sent.at[s, l, j], dst_ref=got.at[s, l, j],
            send_sem=row_send.at[s, l, j], recv_sem=row_got.at[s, l, j],
            device_id=device(-offsets[j]), device_id_type=MESH,
        )

    def build_spread(k, _):
        tracer = lax.broadcasted_iota(jnp.int32, (PADDED, narrow), 0)
        column = lax.broadcasted_iota(jnp.int32, (PADDED, narrow), 1) - k * TRACERS
        column = jnp.where(tracer < TRACERS, column, -1)
        spread[pl.ds(pl.multiple_of(k * PADDED, PADDED), PADDED), :] = jnp.where(column == tracer, 1.0, 0.0).astype(BF16)
        return 0

    lax.fori_loop(0, NODES, build_spread, 0)
    same[...] = jnp.where(
        lax.broadcasted_iota(jnp.int32, (128, 128), 0) == lax.broadcasted_iota(jnp.int32, (128, 128), 1), 1.0, 0.0
    ).astype(BF16)

    loads[0].wait()

    def build_table(l, _):
        own = tracers[l]
        high = high_part(own)
        parts = jnp.concatenate([high, own - high], axis=0).astype(BF16)
        table[0, l, :, 0:own_lanes] = transposed_dot(spread[...], parts).astype(BF16)
        return 0

    for l in range(levels):
        build_table(l, 0)

    def send_rows(s, l):
        lane = lax.broadcasted_iota(jnp.int32, (remote, own_lanes), 1) % elements
        choice = jnp.where(rows_asked[...] == lane, 1.0, 0.0).astype(BF16)
        chosen = transposed_dot(choice, table[s, l, :, 0:own_lanes])
        for j in range(sides):
            sent[s, l, j] = chosen[j * cap : (j + 1) * cap, :]
        for j in range(sides):
            row_copy(s, l, j).start()

    for copy in wishes:
        copy.wait_recv()
    for j in range(sides):
        rows_asked[j * cap : (j + 1) * cap, :] = asked[j]

    def first_rows(l, _):
        send_rows(0, l)
        return 0

    for l in range(levels):
        first_rows(l, 0)

    slot_ids[0:own_lanes, :] = lax.broadcasted_iota(jnp.int32, (own_lanes, 256), 0) % elements
    slot_ids[own_lanes:, :] = jnp.full((256 - own_lanes, 256), -1, jnp.int32)
    for j in range(sides):
        for c in range(cap):
            slot = j * cap + c
            live = jnp.where(c < counts[0, j], elements + slot, -1)
            line = jnp.full((1, 256), live, jnp.int32)
            for part in range(2):
                at = own_lanes + part * remote + slot
                slot_ids[at : at + 1, :] = line

    loads[1].wait()
    loads[2].wait()

    def build_picks(l, _):
        base = l * NODES
        first = departure[pl.ds(base, half), :]
        second = departure[pl.ds(base + half, half), :]
        both = jnp.concatenate([first, second], axis=1)
        for q in range(half // 2):
            target = jnp.concatenate([both[2 * q : 2 * q + 1, :], both[2 * q + 1 : 2 * q + 2, :]], axis=1)
            picks[l, q] = jnp.where(slot_ids[...] == target, 1.0, 0.0).astype(BF16)
        for s in range(substeps):
            matrix = weights[s, l]
            mats[s, l] = jnp.transpose(jnp.concatenate([matrix[:, : half * NODES], matrix[:, half * NODES :]], axis=0))
        return 0

    for l in range(levels):
        build_picks(l, 0)

    left = lax.broadcasted_iota(jnp.int32, (PADDED, own_lanes), 1) < elements

    def one_level(turn, _):
        s, l = turn // levels, turn % levels
        for j in range(sides):
            row_copy(s, l, j).wait_recv()
        for j in range(sides):
            rows[j * cap : (j + 1) * cap, :] = got[s, l, j]
        fetched = rows[...]
        high = high_part(fetched)
        low = fetched - high
        parts = jnp.concatenate([high, low, high, low], axis=0).astype(BF16)
        for at in range(0, wide, 128):
            table[s, l, at : at + 128, own_lanes:] = transposed_dot(same[...], parts[:, at : at + 128]).astype(BF16)

        def one_pair(q, _):
            gathered = jnp.dot(table[s, l], picks[l, q], preferred_element_type=F32)
            for side in range(2):
                c = 2 * q + side
                matrix = mats[s, l, pl.ds(c * NODES, NODES), :]
                value = lowest = highest = None
                for k in range(NODES):
                    item = gathered[k * PADDED : (k + 1) * PADDED, side * 128 : (side + 1) * 128]
                    term = matrix[k : k + 1, :] * item
                    value = term if k == 0 else value + term
                    lowest = item if k == 0 else jnp.minimum(lowest, item)
                    highest = item if k == 0 else jnp.maximum(highest, item)
                value = jnp.clip(value, lowest, highest)
                other = pltpu.roll(value, elements, 1)
                value_high, other_high = high_part(value), high_part(other)
                near = c * PADDED
                past = (c + half) * PADDED
                table[s + 1, l, pl.ds(near, PADDED), 0:own_lanes] = jnp.where(left, value_high, other - other_high).astype(BF16)
                table[s + 1, l, pl.ds(past, PADDED), 0:own_lanes] = jnp.where(left, other_high, value - value_high).astype(BF16)
            return 0

        for q in range(half // 2):
            one_pair(q, 0)

        if s + 1 < substeps:
            send_rows(s + 1, l)

        else:
            packed = lax.dot_general(
                table[s + 1, l, :, 0:own_lanes], spread[...], (((0,), (0,)), ((), ())), preferred_element_type=F32
            )
            out[l] = packed[:elements, :] + packed[elements:, :]
            pltpu.make_async_copy(out.at[l], out_far.at[l], stored.at[l]).start()

        return 0

    for turn in range(substeps * levels):
        one_level(turn, 0)

    for copy in wishes:
        copy.wait_send()
    for s in range(substeps):
        for l in range(levels):
            for j in range(sides):
                row_copy(s, l, j).wait_send()
    for l in range(levels):
        pltpu.make_async_copy(out.at[l], out_far.at[l], stored.at[l]).wait()


def on_device(tracers, weights, departure, needs, counts):
    substeps, elements, levels, _ = weights.shape
    sides, cap = needs.shape[1:]
    wide = NODES * PADDED
    far = pl.BlockSpec(memory_space=pl.ANY)
    smem = pl.BlockSpec(memory_space=pltpu.SMEM)
    result = pl.pallas_call(
        kernel,
        out_shape=jax.ShapeDtypeStruct((levels, elements, NODES * TRACERS), F32),
        in_specs=[far, far, far, smem, smem],
        out_specs=far,
        scratch_shapes=[
            pltpu.VMEM((levels, elements, NODES * TRACERS), F32),
            pltpu.VMEM((substeps, levels, elements, NODES * NODES), F32),
            pltpu.VMEM((levels * NODES, elements), jnp.int32),
            pltpu.VMEM((levels, elements, NODES * TRACERS), F32),
            pltpu.VMEM((substeps + 1, levels, wide, 256), BF16),
            pltpu.VMEM((levels, NODES * elements // 256, 256, 256), BF16),
            pltpu.VMEM((substeps, levels, NODES * NODES // 2, 2 * elements), F32),
            pltpu.VMEM((256, 256), jnp.int32),
            pltpu.VMEM((sides, cap, 128), jnp.int32),
            pltpu.VMEM((sides, cap, 128), jnp.int32),
            pltpu.VMEM((sides * cap, wide), F32),
            pltpu.VMEM((sides * cap, 128), jnp.int32),
            pltpu.VMEM((substeps, levels, sides, cap, wide), F32),
            pltpu.VMEM((substeps, levels, sides, cap, wide), F32),
            pltpu.VMEM((wide, NODES * TRACERS), BF16),
            pltpu.VMEM((128, 128), BF16),
            pltpu.SemaphoreType.DMA((sides,)),
            pltpu.SemaphoreType.DMA((sides,)),
            pltpu.SemaphoreType.DMA((substeps, levels, sides)),
            pltpu.SemaphoreType.DMA((substeps, levels, sides)),
            pltpu.SemaphoreType.DMA((3,)),
            pltpu.SemaphoreType.DMA((levels,)),
        ],
        compiler_params=pltpu.CompilerParams(collective_id=0, has_side_effects=True, vmem_limit_bytes=60 << 20),
    )(
        jnp.transpose(tracers, (1, 0, 2)),
        jnp.transpose(weights, (0, 2, 1, 3)),
        jnp.transpose(departure),
        jnp.transpose(needs, (0, 2, 1)),
        counts,
    )
    return jnp.transpose(result, (1, 0, 2))


def solution(mesh):
    return jax.shard_map(
        on_device,
        mesh=mesh,
        in_specs=(
            P("sfc", None, None),
            P(None, "sfc", None, None),
            P("sfc", None),
            P("sfc", None, None),
            P("sfc", None),
        ),
        out_specs=P("sfc", None, None),
        check_vma=False,
    )
```

profile of v0, /device:TPU:0, one launch (start us, length us, event | category | flops | bytes accessed | tf_op | source)
XLA Modules:
  0.0 27.5 jit_solution(5091094514572574874)
XLA Ops:
  0.0 25.7 %shard_map.55 = f32[3,64,480]{2,1,0:T(8,128)} custom-call(f32[3,64,480]{2,1,0:T(8,128)} %bitcast.6, f32[2,3,64,256]{3,2,1,0:T(8,128)} %bitcast.7, s32[48,64]{1,0:T(8,128)} %bitcast.8, s32[1,4,8]{2,1,0:T(4,128)} %bitcast.9, s32[1,8]{1,0:T(1,128)} %counts.1), custom_call_target="tpu_custom_call" | custom-call | tf_op jit(solution)/shard_map/pallas_call | solution.py:225
  25.7 1.8 %copy.7 = f32[64,3,480]{2,0,1:T(8,128)} copy(f32[64,3,480]{2,0,1:T(8,128)} %bitcast.5) | data formatting | bytes 737280
where the time goes:
time: 27.7 us; the launch traced here: 27.5 us
  Pallas kernels  25.7 us (93%)
  local copies, waits for them, and re-layouts  1.77 us (6%)
    pallas_call x1, Pallas kernels, on_device(): pl.pallas_call(kernel, out_shape=jax.ShapeDtypeStruct((levels, elements,...  25.7 us
    unnamed x1, local copies, waits for them, and re-layouts  1.77 us

commit v1 on v0

v1 whole, which is shorter than its diff:
```python
import jax
import jax.numpy as jnp
from jax import lax
from jax.experimental import pallas as pl
from jax.experimental.pallas import tpu as pltpu
from jax.sharding import PartitionSpec as P

NODES = 16
TRACERS = 30
PADDED = 32
LANES = 128
MESH = pl.DeviceIdType.MESH
F32 = jnp.float32


def kernel(
    tracers_far, weights_far, departure_far, needs_far, counts_far, out,
    tracers, weights, departure, wish, counts, asked, live, mats, state, table, turned,
    sent, got, wish_send, wish_got, row_send, row_got, loaded,
):
    count = lax.axis_size("sfc")
    me = lax.axis_index("sfc")
    substeps, levels, elements, _ = weights.shape
    sides, cap = asked.shape[0], asked.shape[1]
    reach = sides // 2
    narrow = NODES * TRACERS
    remote = sides * cap
    half = NODES // 2
    slots = elements + remote

    def offset_of(j):
        return j - reach + jnp.where(j < reach, 0, 1)

    def device(offset):
        return (lax.rem(me + offset + count, count),)

    barrier = pltpu.get_barrier_semaphore()
    for j in range(sides):
        o = j - reach if j < reach else j - reach + 1
        pl.semaphore_signal(barrier, inc=1, device_id=device(o), device_id_type=MESH)

    loads = [
        pltpu.make_async_copy(far, near, loaded.at[i])
        for i, (far, near) in enumerate((
            (needs_far.at[0], wish), (tracers_far, tracers), (departure_far, departure), (weights_far, weights),
            (counts_far, counts),
        ))
    ]
    for load in loads:
        load.start()

    def wish_copy(j):
        return pltpu.make_async_remote_copy(
            src_ref=wish, dst_ref=asked.at[j],
            send_sem=wish_send.at[j], recv_sem=wish_got.at[j],
            device_id=device(offset_of(j)), device_id_type=MESH,
        )

    def row_copy(s, l, j):
        return pltpu.make_async_remote_copy(
            src_ref=sent.at[s, l, j], dst_ref=got.at[s, l, j],
            send_sem=row_send.at[s, l, j], recv_sem=row_got.at[s, l, j],
            device_id=device(-offset_of(j)), device_id_type=MESH,
        )

    loads[0].wait()
    pl.semaphore_wait(barrier, sides)
    for j in range(sides):
        wish_copy(j).start()

    loads[1].wait()
    for l in range(levels):
        state[0, l, 0:elements, 0:narrow] = tracers[l]

    last = me >= count - reach
    for step in range(sides):
        j = jnp.where(last, sides - 1 - step, step)
        wish_copy(j).wait_recv()
        for l in range(levels):
            for c in range(cap):
                sent[0, l, j, c : c + 1, :] = tracers[l, pl.ds(asked[j, c, j], 1), :]
        for l in range(levels):
            row_copy(0, l, j).start()

    loads[4].wait()
    for j in range(sides):
        for c in range(cap):
            at = j * cap + c
            live[at : at + 1, :] = jnp.full((1, narrow), jnp.where(c < counts[0, j], 1, 0), jnp.int32)

    loads[2].wait()
    loads[3].wait()
    for s in range(substeps):
        for l in range(levels):
            matrix = weights[s, l]
            mats[s, l] = jnp.transpose(jnp.concatenate([matrix[:, : half * NODES], matrix[:, half * NODES :]], axis=0))

    upper = me >= count // 2

    def one_level(s, l):
        for j in range(sides):
            row_copy(s, l, j).wait_recv()
        for j in range(sides):
            at = j * cap
            state[s, l, elements + at : elements + at + cap, 0:narrow] = jnp.where(
                live[at : at + cap, :] > 0, got[s, l, j], 0.0
            )
        table[l] = jnp.transpose(state[s, l])

        first = departure[pl.ds(l * NODES, half), :]
        second = departure[pl.ds(l * NODES + half, half), :]
        both = jnp.concatenate([first, second], axis=1)
        for c in range(half):
            source = jnp.broadcast_to(both[c : c + 1, :], (PADDED, LANES))
            value = lowest = highest = None
            for k in range(NODES):
                item = jnp.take_along_axis(
                    table[l, k * TRACERS : k * TRACERS + PADDED, :], source, axis=1, mode="promise_in_bounds"
                )
                term = mats[s, l, c * NODES + k : c * NODES + k + 1, :] * item
                value = term if k == 0 else value + term
                lowest = item if k == 0 else jnp.minimum(lowest, item)
                highest = item if k == 0 else jnp.maximum(highest, item)
            turned[l, c * TRACERS : c * TRACERS + PADDED, :] = jnp.clip(value, lowest, highest)
        result = jnp.transpose(turned[l])
        near, past = result[:elements, : half * TRACERS], result[elements:, : half * TRACERS]
        if s + 1 < substeps:
            state[s + 1, l, 0:elements, 0 : half * TRACERS] = near
            state[s + 1, l, 0:elements, half * TRACERS : narrow] = past
            for j in range(sides):
                for c in range(cap):
                    sent[s + 1, l, j, c : c + 1, :] = state[s + 1, l, pl.ds(asked[j, c, j], 1), 0:narrow]
            for step in range(sides):
                row_copy(s + 1, l, jnp.where(upper, step, sides - 1 - step)).start()
        else:
            out[l, :, 0 : half * TRACERS] = near
            out[l, :, half * TRACERS : narrow] = past

    for s in range(substeps):
        for l in range(levels):
            one_level(s, l)

    for j in range(sides):
        wish_copy(j).wait_send()
    for s in range(substeps):
        for l in range(levels):
            for j in range(sides):
                row_copy(s, l, j).wait_send()


def on_device(tracers, weights, departure, needs, counts):
    substeps, elements, levels, _ = weights.shape
    sides, cap = needs.shape[1:]
    narrow = NODES * TRACERS
    wide = NODES * PADDED
    half = NODES // 2
    far = pl.BlockSpec(memory_space=pl.ANY)
    result = pl.pallas_call(
        kernel,
        out_shape=pltpu.VMEM((levels, elements, narrow), F32),
        in_specs=[far] * 5,
        out_specs=pl.BlockSpec(memory_space=pltpu.VMEM),
        scratch_shapes=[
            pltpu.VMEM((levels, elements, narrow), F32),
            pltpu.VMEM((substeps, levels, elements, NODES * NODES), F32),
            pltpu.VMEM((levels * NODES, elements), jnp.int32),
            pltpu.SMEM((cap, sides), jnp.int32),
            pltpu.SMEM((1, sides), jnp.int32),
            pltpu.SMEM((sides, cap, sides), jnp.int32),
            pltpu.VMEM((sides * cap, narrow), jnp.int32),
            pltpu.VMEM((substeps, levels, half * NODES, 2 * elements), F32),
            pltpu.VMEM((substeps, levels, LANES, wide), F32),
            pltpu.VMEM((levels, wide, LANES), F32),
            pltpu.VMEM((levels, half * PADDED, 2 * elements), F32),
            pltpu.VMEM((substeps, levels, sides, cap, narrow), F32),
            pltpu.VMEM((substeps, levels, sides, cap, narrow), F32),
            pltpu.SemaphoreType.DMA((sides,)),
            pltpu.SemaphoreType.DMA((sides,)),
            pltpu.SemaphoreType.DMA((substeps, levels, sides)),
            pltpu.SemaphoreType.DMA((substeps, levels, sides)),
            pltpu.SemaphoreType.DMA((5,)),
        ],
        compiler_params=pltpu.CompilerParams(collective_id=0, has_side_effects=True, vmem_limit_bytes=60 << 20),
    )(
        jnp.transpose(tracers, (1, 0, 2)),
        jnp.transpose(weights, (0, 2, 1, 3)),
        jnp.transpose(departure),
        jnp.transpose(needs, (0, 2, 1)),
        counts,
    )
    return jnp.transpose(result, (1, 0, 2))


def solution(mesh):
    return jax.shard_map(
        on_device,
        mesh=mesh,
        in_specs=(
            P("sfc", None, None),
            P(None, "sfc", None, None),
            P("sfc", None),
            P("sfc", None, None),
            P("sfc", None),
        ),
        out_specs=P("sfc", None, None),
        check_vma=False,
    )
```

time: 27.7 us -> 25.8 us (0.931)
  local copies, waits for them, and re-layouts: 1.77 us -> 0.75 us
  Pallas kernels: 25.7 us -> 24.9 us
    unnamed x1, local copies, waits for them, and re-layouts: 1.77 us -> 0.75 us
    pallas_call x1, Pallas kernels: 25.7 us -> 24.9 us  [on_device(): pl.pallas_call(kernel, out_shape=pltpu.VMEM((levels, elements, narrow), F...]
where the time goes in v1:
time: 25.8 us; the launch traced here: 25.6 us
  Pallas kernels  24.9 us (97%)
  local copies, waits for them, and re-layouts  0.75 us (3%)
    pallas_call x1, Pallas kernels, on_device(): pl.pallas_call(kernel, out_shape=pltpu.VMEM((levels, elements, narrow), F...  24.9 us
    unnamed x1, local copies, waits for them, and re-layouts  0.75 us

profile of v1, /device:TPU:0, one launch (start us, length us, event | category | flops | bytes accessed | tf_op | source)
XLA Modules:
  0.0 25.6 jit_solution(16547126651062421436)
XLA Ops:
  0.0 24.9 %shard_map.55 = f32[3,64,480]{2,1,0:T(8,128)S(1)} custom-call(f32[3,64,480]{2,1,0:T(8,128)} %bitcast.6, f32[2,3,64,256]{3,2,1,0:T(8,128)} %bitcast.7, s32[48,64]{1,0:T(8,128)} %bitcast.8, s32[1,4,8]{2,1,0:T(4,128)} %bitcast.9, s32[1,8]{1,0:T(1,128)} %counts_far.1), custom_call_target="tpu_custom_call" | custom-call | tf_op jit(solution)/shard_map/pallas_call | solution.py:158
  24.9 0.7 %copy.7 = f32[64,3,480]{2,0,1:T(8,128)} copy(f32[64,3,480]{2,0,1:T(8,128)S(1)} %bitcast.5) | data formatting | bytes 737280

commit v2 on v1

--- a/solution.py
+++ b/solution.py
@@ -11,11 +11,13 @@
 LANES = 128
 MESH = pl.DeviceIdType.MESH
 F32 = jnp.float32
+BF16 = jnp.bfloat16
+DENSE = 8
 
 
 def kernel(
     tracers_far, weights_far, departure_far, needs_far, counts_far, out,
-    tracers, weights, departure, wish, counts, asked, live, mats, state, table, turned,
+    tracers, weights, departure, wish, counts, asked, live, mats, state, table, turned, parts, picks,
     sent, got, wish_send, wish_got, row_send, row_got, loaded,
 ):
     count = lax.axis_size("sfc")
@@ -52,14 +54,14 @@
     def wish_copy(j):
         return pltpu.make_async_remote_copy(
             src_ref=wish, dst_ref=asked.at[j],
-            send_sem=wish_send.at[j], recv_sem=wish_got.at[j],
+            send_sem=wish_send, recv_sem=wish_got.at[j],
             device_id=device(offset_of(j)), device_id_type=MESH,
         )
 
     def row_copy(s, l, j):
         return pltpu.make_async_remote_copy(
             src_ref=sent.at[s, l, j], dst_ref=got.at[s, l, j],
-            send_sem=row_send.at[s, l, j], recv_sem=row_got.at[s, l, j],
+            send_sem=row_send, recv_sem=row_got.at[s, l],
             device_id=device(-offset_of(j)), device_id_type=MESH,
         )
 
@@ -72,15 +74,26 @@
     for l in range(levels):
         state[0, l, 0:elements, 0:narrow] = tracers[l]
 
-    last = me >= count - reach
+    past_low = count - 1 - me
+
+    def arrival(step):
+        low = jnp.where(step <= me, step, jnp.where(step <= reach, step + reach - 1, me + step - reach))
+        high = jnp.where(step <= reach - 1 + past_low, sides - 1 - step, step - reach - past_low)
+        return jnp.where(me < reach, low, jnp.where(past_low < reach, high, step))
+
     for step in range(sides):
-        j = jnp.where(last, sides - 1 - step, step)
+        j = arrival(step)
         wish_copy(j).wait_recv()
         for l in range(levels):
             for c in range(cap):
                 sent[0, l, j, c : c + 1, :] = tracers[l, pl.ds(asked[j, c, j], 1), :]
         for l in range(levels):
             row_copy(0, l, j).start()
+
+    def targets(l):
+        first = departure[pl.ds(l * NODES, half), :]
+        second = departure[pl.ds(l * NODES + half, half), :]
+        return jnp.concatenate([first, second], axis=1)
 
     loads[4].wait()
     for j in range(sides):
@@ -89,6 +102,16 @@
             live[at : at + 1, :] = jnp.full((1, narrow), jnp.where(c < counts[0, j], 1, 0), jnp.int32)
 
     loads[2].wait()
+    for s in range(substeps):
+        for l in range(levels):
+            state[s, l, slots:, :] = jnp.zeros((LANES - slots, NODES * PADDED), F32)
+    if DENSE:
+        slot_ids = lax.broadcasted_iota(jnp.int32, (2 * LANES, 2 * LANES), 0) % LANES
+        for l in range(levels):
+            both = targets(l)
+            for q in range(DENSE // 2):
+                target = jnp.concatenate([both[2 * q : 2 * q + 1, :], both[2 * q + 1 : 2 * q + 2, :]], axis=1)
+                picks[l, q] = jnp.where(slot_ids == target, 1.0, 0.0).astype(BF16)
     loads[3].wait()
     for s in range(substeps):
         for l in range(levels):
@@ -97,31 +120,49 @@
 
     upper = me >= count // 2
 
-    def one_level(s, l):
-        for j in range(sides):
-            row_copy(s, l, j).wait_recv()
+
+    def reduce(s, l, c, items):
+        value = lowest = highest = None
+        for k in range(NODES):
+            item = items(k)
+            term = mats[s, l, c * NODES + k : c * NODES + k + 1, :] * item
+            value = term if k == 0 else value + term
+            lowest = item if k == 0 else jnp.minimum(lowest, item)
+            highest = item if k == 0 else jnp.maximum(highest, item)
+        turned[l, c * TRACERS : c * TRACERS + PADDED, :] = jnp.clip(value, lowest, highest)
+
+    def receive(s, l):
+        pltpu.make_async_remote_copy(
+            src_ref=sent.at[s, l], dst_ref=got.at[s, l], send_sem=row_send, recv_sem=row_got.at[s, l],
+            device_id=device(1), device_id_type=MESH,
+        ).wait_recv()
+
+    def arrange(s, l):
         for j in range(sides):
             at = j * cap
             state[s, l, elements + at : elements + at + cap, 0:narrow] = jnp.where(
                 live[at : at + cap, :] > 0, got[s, l, j], 0.0
             )
         table[l] = jnp.transpose(state[s, l])
-
-        first = departure[pl.ds(l * NODES, half), :]
-        second = departure[pl.ds(l * NODES + half, half), :]
-        both = jnp.concatenate([first, second], axis=1)
-        for c in range(half):
+        for k in range(NODES if DENSE else 0):
+            block = table[l, k * TRACERS : k * TRACERS + PADDED, :]
+            high = block.astype(BF16)
+            parts[l, k * PADDED : (k + 1) * PADDED, 0:LANES] = high
+            parts[l, k * PADDED : (k + 1) * PADDED, LANES:] = (block - high.astype(F32)).astype(BF16)
+
+    def gather(s, l):
+        for q in range(DENSE // 2):
+            gathered = jnp.dot(parts[l], picks[l, q], preferred_element_type=F32)
+            for side in range(2):
+                reduce(s, l, 2 * q + side, lambda k: gathered[k * PADDED : (k + 1) * PADDED, side * LANES : (side + 1) * LANES])
+        both = targets(l)
+        for c in range(DENSE, half):
             source = jnp.broadcast_to(both[c : c + 1, :], (PADDED, LANES))
-            value = lowest = highest = None
-            for k in range(NODES):
-                item = jnp.take_along_axis(
-                    table[l, k * TRACERS : k * TRACERS + PADDED, :], source, axis=1, mode="promise_in_bounds"
-                )
-                term = mats[s, l, c * NODES + k : c * NODES + k + 1, :] * item
-                value = term if k == 0 else value + term
-                lowest = item if k == 0 else jnp.minimum(lowest, item)
-                highest = item if k == 0 else jnp.maximum(highest, item)
-            turned[l, c * TRACERS : c * TRACERS + PADDED, :] = jnp.clip(value, lowest, highest)
+            reduce(s, l, c, lambda k: jnp.take_along_axis(
+                table[l, k * TRACERS : k * TRACERS + PADDED, :], source, axis=1, mode="promise_in_bounds"
+            ))
+
+    def finish(s, l):
         result = jnp.transpose(turned[l])
         near, past = result[:elements, : half * TRACERS], result[elements:, : half * TRACERS]
         if s + 1 < substeps:
@@ -130,22 +171,31 @@
             for j in range(sides):
                 for c in range(cap):
                     sent[s + 1, l, j, c : c + 1, :] = state[s + 1, l, pl.ds(asked[j, c, j], 1), 0:narrow]
-            for step in range(sides):
-                row_copy(s + 1, l, jnp.where(upper, step, sides - 1 - step)).start()
         else:
             out[l, :, 0 : half * TRACERS] = near
             out[l, :, half * TRACERS : narrow] = past
 
+    def send(s, l):
+        if s + 1 < substeps:
+            for step in range(sides):
+                row_copy(s + 1, l, jnp.where(upper, step, sides - 1 - step)).start()
+
     for s in range(substeps):
         for l in range(levels):
-            one_level(s, l)
-
-    for j in range(sides):
-        wish_copy(j).wait_send()
-    for s in range(substeps):
-        for l in range(levels):
-            for j in range(sides):
-                row_copy(s, l, j).wait_send()
+            receive(s, l)
+            arrange(s, l)
+            gather(s, l)
+            finish(s, l)
+            send(s, l)
+
+    pltpu.make_async_remote_copy(
+        src_ref=asked, dst_ref=asked, send_sem=wish_send, recv_sem=wish_got.at[0],
+        device_id=device(1), device_id_type=MESH,
+    ).wait_send()
+    pltpu.make_async_remote_copy(
+        src_ref=sent, dst_ref=got, send_sem=row_send, recv_sem=row_got.at[0, 0],
+        device_id=device(1), device_id_type=MESH,
+    ).wait_send()
 
 
 def on_device(tracers, weights, departure, needs, counts):
@@ -172,12 +222,14 @@
             pltpu.VMEM((substeps, levels, LANES, wide), F32),
             pltpu.VMEM((levels, wide, LANES), F32),
             pltpu.VMEM((levels, half * PADDED, 2 * elements), F32),
+            pltpu.VMEM((levels, wide, 2 * LANES), BF16),
+            pltpu.VMEM((levels, max(DENSE // 2, 1), 2 * LANES, 2 * LANES), BF16),
             pltpu.VMEM((substeps, levels, sides, cap, narrow), F32),
             pltpu.VMEM((substeps, levels, sides, cap, narrow), F32),
+            pltpu.SemaphoreType.DMA,
             pltpu.SemaphoreType.DMA((sides,)),
-            pltpu.SemaphoreType.DMA((sides,)),
-            pltpu.SemaphoreType.DMA((substeps, levels, sides)),
-            pltpu.SemaphoreType.DMA((substeps, levels, sides)),
+            pltpu.SemaphoreType.DMA,
+            pltpu.SemaphoreType.DMA((substeps, levels)),
             pltpu.SemaphoreType.DMA((5,)),
         ],
         compiler_params=pltpu.CompilerParams(collective_id=0, has_side_effects=True, vmem_limit_bytes=60 << 20),

time: 25.8 us -> 22.9 us (0.89)
  Pallas kernels: 24.9 us -> 22 us
    pallas_call x1, Pallas kernels: 24.9 us -> 22 us  [on_device(): pl.pallas_call(kernel, out_shape=pltpu.VMEM((levels, elements, narrow), F...]
where the time goes in v2:
time: 22.9 us; the launch traced here: 22.8 us
  Pallas kernels  22 us (96%)
  local copies, waits for them, and re-layouts  0.75 us (3%)
    pallas_call x1, Pallas kernels, on_device(): pl.pallas_call(kernel, out_shape=pltpu.VMEM((levels, elements, narrow), F...  22 us
    unnamed x1, local copies, waits for them, and re-layouts  0.75 us

profile of v2, /device:TPU:0, one launch (start us, length us, event | category | flops | bytes accessed | tf_op | source)
XLA Modules:
  0.0 22.8 jit_solution(4301467046327607493)
XLA Ops:
  0.0 22.0 %shard_map.55 = f32[3,64,480]{2,1,0:T(8,128)S(1)} custom-call(f32[3,64,480]{2,1,0:T(8,128)} %bitcast.6, f32[2,3,64,256]{3,2,1,0:T(8,128)} %bitcast.7, s32[48,64]{1,0:T(8,128)} %bitcast.8, s32[1,4,8]{2,1,0:T(4,128)} %bitcast.9, s32[1,8]{1,0:T(1,128)} %counts_far.1), custom_call_target="tpu_custom_call" | custom-call | tf_op jit(solution)/shard_map/pallas_call | solution.py:208
  22.0 0.7 %copy.7 = f32[64,3,480]{2,0,1:T(8,128)} copy(f32[64,3,480]{2,0,1:T(8,128)S(1)} %bitcast.5) | data formatting | bytes 737280

commit v3 on v2

v3 whole, which is shorter than its diff:
```python
import jax
import jax.numpy as jnp
from jax import lax
from jax.experimental import pallas as pl
from jax.experimental.pallas import tpu as pltpu
from jax.sharding import PartitionSpec as P

NODES = 16
TRACERS = 30
PADDED = 32
LANES = 128
MESH = pl.DeviceIdType.MESH
F32 = jnp.float32
BF16 = jnp.bfloat16


def kernel(
    tracers_far, weights_far, departure_far, needs_far, counts_far, out,
    tracers, weights, departure, wish, counts, asked, slot_ids, mats, state, table, turned, turned_past, parts, picks,
    sent_first, got_first, sent, got, wish_send, wish_got, row_send, row_got, loaded,
):
    count = lax.axis_size("sfc")
    me = lax.axis_index("sfc")
    substeps, levels, elements, _ = weights.shape
    sides, cap = asked.shape[0], asked.shape[1]
    reach = sides // 2
    narrow = NODES * TRACERS
    remote = sides * cap
    half = NODES // 2
    slots = elements + remote

    def offset_of(j):
        return j - reach + jnp.where(j < reach, 0, 1)

    def device(offset):
        return (lax.rem(me + offset + count, count),)

    loads = [
        pltpu.make_async_copy(far, near, loaded.at[i])
        for i, (far, near) in enumerate((
            (needs_far.at[0], wish), (tracers_far, tracers), (departure_far, departure), (weights_far, weights),
            (counts_far, counts),
        ))
    ]
    loads[0].start()

    barrier = pltpu.get_barrier_semaphore()
    for j in range(sides):
        o = j - reach if j < reach else j - reach + 1
        pl.semaphore_signal(barrier, inc=1, device_id=device(o), device_id_type=MESH)

    for load in loads[1:]:
        load.start()

    def wish_copy(j):
        return pltpu.make_async_remote_copy(
            src_ref=wish, dst_ref=asked.at[j],
            send_sem=wish_send, recv_sem=wish_got.at[j],
            device_id=device(offset_of(j)), device_id_type=MESH,
        )

    def ends(s):
        return (sent_first, got_first) if s == 0 else (sent.at[s - 1], got.at[s - 1])

    def row_copy(s, l, j):
        source, target = ends(s)
        return pltpu.make_async_remote_copy(
            src_ref=source.at[l, j], dst_ref=target.at[l, j], send_sem=row_send.at[s], recv_sem=row_got.at[s, l],
            device_id=device(-offset_of(j)), device_id_type=MESH,
        )

    def rows_of(s, l):
        source, target = ends(s)
        return pltpu.make_async_remote_copy(
            src_ref=source.at[l], dst_ref=target.at[l], send_sem=row_send.at[s], recv_sem=row_got.at[s, l],
            device_id=device(1), device_id_type=MESH,
        )

    loads[0].wait()
    pl.semaphore_wait(barrier, sides)
    upper = me >= count // 2
    for step in range(sides):
        wish_copy(jnp.where(upper, sides - 1 - step, step)).start()

    loads[1].wait()
    for l in range(levels):
        state[0, l, 0:elements, 0:narrow] = tracers[l]

    past_low = count - 1 - me

    def arrival(step):
        low = jnp.where(step <= me, step, jnp.where(step <= reach, step + reach - 1, me + step - reach))
        high = jnp.where(step <= reach - 1 + past_low, sides - 1 - step, step - reach - past_low)
        return jnp.where(me < reach, low, jnp.where(past_low < reach, high, step))

    for step in range(sides):
        j = arrival(step)
        wish_copy(j).wait_recv()
        for l in range(levels):
            for c in range(cap):
                sent_first[l, j, c : c + 1, :] = tracers[l, pl.ds(asked[j, c, j], 1), :]
        for l in range(levels):
            row_copy(0, l, j).start()

    def targets(l):
        first = departure[pl.ds(l * NODES, half), :]
        second = departure[pl.ds(l * NODES + half, half), :]
        return jnp.concatenate([first, second], axis=1)

    def targets(l):
        first = departure[pl.ds(l * NODES, half), :]
        second = departure[pl.ds(l * NODES + half, half), :]
        return jnp.concatenate([first, second], axis=1)

    loads[4].wait()
    slot_ids[...] = lax.broadcasted_iota(jnp.int32, (LANES, 2 * LANES), 0)
    for j in range(sides):
        for c in range(cap):
            at = elements + j * cap + c
            slot_ids[at : at + 1, :] = jnp.full((1, 2 * LANES), jnp.where(c < counts[0, j], at, -1), jnp.int32)

    loads[2].wait()
    for s in range(substeps):
        for l in range(levels):
            state[s, l, slots:, :] = jnp.zeros((LANES - slots, NODES * PADDED), F32)
    for l in range(levels):
        both = targets(l)
        for q in range(half // 2):
            target = jnp.concatenate([both[2 * q : 2 * q + 1, :], both[2 * q + 1 : 2 * q + 2, :]], axis=1)
            pick = jnp.where(slot_ids[...] == target, 1.0, 0.0).astype(BF16)
            picks[l, q, 0:LANES, :] = pick
            picks[l, q, LANES:, :] = pick
    loads[3].wait()
    for s in range(substeps):
        for l in range(levels):
            matrix = weights[s, l]
            mats[s, l] = jnp.transpose(jnp.concatenate([matrix[:, : half * NODES], matrix[:, half * NODES :]], axis=0))

    shift = half * TRACERS % LANES

    def reduce(s, l, c, items):
        value = lowest = highest = None
        for k in range(NODES):
            item = items(k)
            term = mats[s, l, c * NODES + k : c * NODES + k + 1, :] * item
            value = term if k == 0 else value + term
            lowest = item if k == 0 else jnp.minimum(lowest, item)
            highest = item if k == 0 else jnp.maximum(highest, item)
        value = jnp.clip(value, lowest, highest)
        if s + 1 < substeps:
            turned[l, c * PADDED : (c + 1) * PADDED, :] = value
        else:
            turned[l, c * TRACERS : c * TRACERS + PADDED, :] = value
            at = shift + c * TRACERS
            turned_past[l, at : at + PADDED, :] = value

    def receive(s, l):
        rows_of(s, l).wait_recv()

    def arrange(s, l):
        pitch, lanes = (TRACERS, narrow) if s == 0 else (PADDED, NODES * PADDED)
        for j in range(sides):
            at = elements + j * cap
            state[s, l, at : at + cap, 0:lanes] = ends(s)[1][l, j]
        table[l] = jnp.transpose(state[s, l])
        for k in range(NODES):
            block = table[l, k * pitch : k * pitch + PADDED, :]
            high = block.astype(BF16)
            parts[l, k * PADDED : (k + 1) * PADDED, 0:LANES] = high
            parts[l, k * PADDED : (k + 1) * PADDED, LANES:] = (block - high.astype(F32)).astype(BF16)

    def gather(s, l):
        for q in range(half // 2):
            gathered = jnp.dot(parts[l], picks[l, q], preferred_element_type=F32)
            for side in range(2):
                reduce(s, l, 2 * q + side, lambda k: gathered[k * PADDED : (k + 1) * PADDED, side * LANES : (side + 1) * LANES])

    def finish(s, l):
        result = jnp.transpose(turned[l])
        if s + 1 < substeps:
            middle = half * PADDED
            state[s + 1, l, 0:elements, 0:middle] = result[:elements]
            state[s + 1, l, 0:elements, middle:] = result[elements:]
            for j in range(sides):
                for c in range(cap):
                    sent[s, l, j, c : c + 1, :] = state[s + 1, l, pl.ds(asked[j, c, j], 1), :]
        else:
            middle = half * TRACERS
            out[l, :, 0:middle] = result[:elements, :middle]
            out[l, :, middle:narrow] = jnp.transpose(turned_past[l])[elements:, shift : shift + narrow - middle]

    def send(s, l):
        if s + 1 < substeps:
            for step in range(sides):
                row_copy(s + 1, l, jnp.where(upper, step, sides - 1 - step)).start()

    for s in range(substeps):
        receive(s, 0)
        arrange(s, 0)
        for l in range(levels):
            gather(s, l)
            if l + 1 < levels:
                receive(s, l + 1)
                arrange(s, l + 1)
            finish(s, l)
            send(s, l)

    pltpu.make_async_remote_copy(
        src_ref=asked, dst_ref=asked, send_sem=wish_send, recv_sem=wish_got.at[0],
        device_id=device(1), device_id_type=MESH,
    ).wait_send()
    for s in range(substeps):
        source, target = ends(s)
        pltpu.make_async_remote_copy(
            src_ref=source, dst_ref=target, send_sem=row_send.at[s], recv_sem=row_got.at[s, 0],
            device_id=device(1), device_id_type=MESH,
        ).wait_send()


def on_device(tracers, weights, departure, needs, counts):
    substeps, elements, levels, _ = weights.shape
    sides, cap = needs.shape[1:]
    narrow = NODES * TRACERS
    wide = NODES * PADDED
    half = NODES // 2
    far = pl.BlockSpec(memory_space=pl.ANY)
    result = pl.pallas_call(
        kernel,
        out_shape=pltpu.VMEM((levels, elements, narrow), F32),
        in_specs=[far] * 5,
        out_specs=pl.BlockSpec(memory_space=pltpu.VMEM),
        scratch_shapes=[
            pltpu.VMEM((levels, elements, narrow), F32),
            pltpu.VMEM((substeps, levels, elements, NODES * NODES), F32),
            pltpu.VMEM((levels * NODES, elements), jnp.int32),
            pltpu.VMEM((cap, sides), jnp.int32),
            pltpu.SMEM((1, sides), jnp.int32),
            pltpu.SMEM((sides, cap, sides), jnp.int32),
            pltpu.VMEM((LANES, 2 * LANES), jnp.int32),
            pltpu.VMEM((substeps, levels, half * NODES, 2 * elements), F32),
            pltpu.VMEM((substeps, levels, LANES, wide), F32),
            pltpu.VMEM((levels, wide, LANES), F32),
            pltpu.VMEM((levels, half * PADDED, 2 * elements), F32),
            pltpu.VMEM((levels, 3 * LANES, 2 * elements), F32),
            pltpu.VMEM((levels, wide, 2 * LANES), BF16),
            pltpu.VMEM((levels, half // 2, 2 * LANES, 2 * LANES), BF16),
            pltpu.VMEM((levels, sides, cap, narrow), F32),
            pltpu.VMEM((levels, sides, cap, narrow), F32),
            pltpu.VMEM((substeps - 1, levels, sides, cap, wide), F32),
            pltpu.VMEM((substeps - 1, levels, sides, cap, wide), F32),
            pltpu.SemaphoreType.DMA,
            pltpu.SemaphoreType.DMA((sides,)),
            pltpu.SemaphoreType.DMA((substeps,)),
            pltpu.SemaphoreType.DMA((substeps, levels)),
            pltpu.SemaphoreType.DMA((5,)),
        ],
        compiler_params=pltpu.CompilerParams(collective_id=0, has_side_effects=True, vmem_limit_bytes=60 << 20),
    )(
        jnp.transpose(tracers, (1, 0, 2)),
        jnp.transpose(weights, (0, 2, 1, 3)),
        jnp.transpose(departure),
        jnp.transpose(needs, (0, 2, 1)),
        counts,
    )
    return jnp.transpose(result, (1, 0, 2))


def solution(mesh):
    return jax.shard_map(
        on_device,
        mesh=mesh,
        in_specs=(
            P("sfc", None, None),
            P(None, "sfc", None, None),
            P("sfc", None),
            P("sfc", None, None),
            P("sfc", None),
        ),
        out_specs=P("sfc", None, None),
        check_vma=False,
    )
```

time: 22.9 us -> 22.5 us (0.983)
  Pallas kernels: 22 us -> 21.6 us
    pallas_call x1, Pallas kernels: 22 us -> 21.6 us  [on_device(): pl.pallas_call(kernel, out_shape=pltpu.VMEM((levels, elements, narrow), F...]
where the time goes in v3:
time: 22.5 us; the launch traced here: 22.3 us
  Pallas kernels  21.6 us (96%)
  local copies, waits for them, and re-layouts  0.75 us (3%)
    pallas_call x1, Pallas kernels, on_device(): pl.pallas_call(kernel, out_shape=pltpu.VMEM((levels, elements, narrow), F...  21.6 us
    unnamed x1, local copies, waits for them, and re-layouts  0.75 us

profile of v3, /device:TPU:0, one launch (start us, length us, event | category | flops | bytes accessed | tf_op | source)
XLA Modules:
  0.0 22.3 jit_solution(9934454974312494002)
XLA Ops:
  0.0 21.6 %shard_map.55 = f32[3,64,480]{2,1,0:T(8,128)S(1)} custom-call(f32[3,64,480]{2,1,0:T(8,128)} %bitcast.6, f32[2,3,64,256]{3,2,1,0:T(8,128)} %bitcast.7, s32[48,64]{1,0:T(8,128)} %bitcast.8, s32[1,4,8]{2,1,0:T(4,128)} %bitcast.9, s32[1,8]{1,0:T(1,128)} %counts_far.1), custom_call_target="tpu_custom_call" | custom-call | tf_op jit(solution)/shard_map/pallas_call | solution.py:227
  21.6 0.7 %copy.7 = f32[64,3,480]{2,0,1:T(8,128)} copy(f32[64,3,480]{2,0,1:T(8,128)S(1)} %bitcast.5) | data formatting | bytes 737280

commit v4 on v3

--- a/solution.py
+++ b/solution.py
@@ -79,8 +79,16 @@
     loads[0].wait()
     pl.semaphore_wait(barrier, sides)
     upper = me >= count // 2
+    across = me - (count - reach)
+
+    def ask(step):
+        return jnp.where(step <= across, sides - 1 - across + step, jnp.where(upper, sides - 1 - step, step))
+
+    def answer(step):
+        return jnp.where(step <= across, across - step, jnp.where(upper, step, sides - 1 - step))
+
     for step in range(sides):
-        wish_copy(jnp.where(upper, sides - 1 - step, step)).start()
+        wish_copy(ask(step)).start()
 
     loads[1].wait()
     for l in range(levels):
@@ -192,16 +200,13 @@
     def send(s, l):
         if s + 1 < substeps:
             for step in range(sides):
-                row_copy(s + 1, l, jnp.where(upper, step, sides - 1 - step)).start()
-
-    for s in range(substeps):
-        receive(s, 0)
-        arrange(s, 0)
-        for l in range(levels):
+                row_copy(s + 1, l, answer(step)).start()
+
+    for s in range(substeps):
+        for l in range(levels):
+            receive(s, l)
+            arrange(s, l)
             gather(s, l)
-            if l + 1 < levels:
-                receive(s, l + 1)
-                arrange(s, l + 1)
             finish(s, l)
             send(s, l)
 

time: 22.5 us -> 22.4 us (level)
  no operation moved by 1% of the time
where the time goes in v4:
time: 22.4 us; the launch traced here: 22.2 us
  Pallas kernels  21.4 us (96%)
  local copies, waits for them, and re-layouts  0.75 us (3%)
    pallas_call x1, Pallas kernels, on_device(): pl.pallas_call(kernel, out_shape=pltpu.VMEM((levels, elements, narrow), F...  21.4 us
    unnamed x1, local copies, waits for them, and re-layouts  0.75 us

profile of v4, /device:TPU:0, one launch (start us, length us, event | category | flops | bytes accessed | tf_op | source)
XLA Modules:
  0.0 22.2 jit_solution(17840493177340925592)
XLA Ops:
  0.0 21.4 %shard_map.55 = f32[3,64,480]{2,1,0:T(8,128)S(1)} custom-call(f32[3,64,480]{2,1,0:T(8,128)} %bitcast.6, f32[2,3,64,256]{3,2,1,0:T(8,128)} %bitcast.7, s32[48,64]{1,0:T(8,128)} %bitcast.8, s32[1,4,8]{2,1,0:T(4,128)} %bitcast.9, s32[1,8]{1,0:T(1,128)} %counts_far.1), custom_call_target="tpu_custom_call" | custom-call | tf_op jit(solution)/shard_map/pallas_call | solution.py:232
  21.4 0.7 %copy.7 = f32[64,3,480]{2,0,1:T(8,128)} copy(f32[64,3,480]{2,0,1:T(8,128)S(1)} %bitcast.5) | data formatting | bytes 737280
